TPU v7x, 16 devices: a whole 2x2x2 slice. The times are simulated.
16 devices in a mesh: tp: 2 (over z), dp: 8 (over y, x, core).
Axes of the slice: x: 2, y: 2, z: 2, core: 2. Of those that a mesh axis runs over, the one named last changes fastest.
Arguments:
- a_mat: bfloat16 [4096, 32768], P(('dp', 'tp'))
- b_mat: bfloat16 [32768, 14336], P(('dp', 'tp'))
Outputs:
- output: bfloat16 [4096, 14336], P(('dp', 'tp'))
All inputs are finite; a program needn't handle non-finite values.
Results may differ from a plain program's by a relative error of at most 0.001.
Values are sent between devices in bfloat16 or wider.
A program may use at most 1 GiB of HBM per device.

v0:
```python
import jax
import jax.numpy as jnp
from jax import lax
from jax.experimental import pallas as pl
from jax.experimental.pallas import tpu as pltpu
from jax.sharding import PartitionSpec as P

MESH = pl.DeviceIdType.MESH
W = 128
C = 2 * W
LOOK = 2
D3 = 6
DO = 6
LATE = 4
AHEAD = 2
LAG = 5
RX, RZ, RC = 2 * LOOK, LOOK + 1, 8
AX, AY, AZ = 0, 1, 2


def bits_of(d):
    return (d // 4, (d // 2) % 2, d % 2)


def counts(columns):
    paired = columns // C // 4
    return columns // C - 2 * paired - 1, paired


def kernel(a_hbm, b_hbm, c_v, bx_hbm, bz_hbm, bxz_hbm, relay,
           a_v, b_v, p_v, r1_v, s2_v, r2_v, s3_v, r3_v, q_v,
           hop_send, own_sem, bx_send, bx_recv, bxz_send, bxz_recv, ch_send, ch_recv, b_sem,
           s1_sem, r1_sem, s2_sem, r2_sem, s3_sem, r3_sem, qs_sem, qr_sem, credit):
    depth, columns = b_hbm.shape
    plain, paired = counts(columns)
    tiles = plain + paired
    rows, upper = a_hbm.shape[0], a_hbm.shape[0] // 2
    half = depth // 2
    chunks = 16 + 2 * paired
    last = plain + paired
    rate = max(114, -(-1600 // plain), -(-100 * (15 + 2 * paired) // (tiles - 1)))

    dp, tp = lax.axis_index("dp"), lax.axis_index("tp")
    core, x, y, z = dp % 2, (dp // 2) % 2, dp // 4, tp

    def flip(v, bit):
        return v + bit - 2 * v * bit

    def device(bits, other=0):
        return {"dp": flip(y, bits[1]) * 4 + flip(x, bits[0]) * 2 + flip(core, other), "tp": flip(z, bits[2])}

    axis_nbr = [device((1, 0, 0)), device((0, 1, 0)), device((0, 0, 1))]
    partner = device((0, 0, 0), 1)

    barrier = pltpu.get_barrier_semaphore()
    for nbr in (*axis_nbr, partner):
        pl.semaphore_signal(barrier, inc=1, device_id=nbr, device_id_type=MESH)

    def send(src, dst, send_sem, recv_sem, to):
        return pltpu.make_async_remote_copy(
            src_ref=src, dst_ref=dst, send_sem=send_sem, recv_sem=recv_sem, device_id=to, device_id_type=MESH)

    def wait_bytes(ref, sem):
        pltpu.make_async_copy(ref, ref, sem).wait()

    def when(t, low, high, fn):
        pl.when(jnp.logical_and(t >= low, t < high))(fn)

    def is_paired(t):
        return (t + tiles - plain) // tiles

    def tile_cols(t, g=None):
        col = t * C + is_paired(t) * ((t - plain) * C + z * C)
        if g is None:
            return pl.ds(pl.multiple_of(col, W), C)
        return pl.ds(pl.multiple_of(col + g * W, W), W)

    def their_cols(q):
        return pl.ds(pl.multiple_of((plain + 2 * q + 1 - z) * C, W), C)

    def last_cols(side):
        return pl.ds(pl.multiple_of((plain + 2 * paired) * C + side * W, W), W)

    def a_cols(bits, h):
        to = device(bits, h)
        return a_hbm.at[:, pl.ds(pl.multiple_of((to["dp"] * 2 + to["tp"]) * depth, depth), depth)]

    def near(d, h):
        return a_v.at[d, :, pl.ds(h * depth, depth)]

    def far(d, h):
        return a_v.at[d, :, pl.ds((2 + h) * depth, depth)]

    def held(i, h):
        return relay.at[i, :, pl.ds(h * depth, depth)]

    def hop(n, h, src, dst, axis):
        return send(src, dst, hop_send, ch_recv.at[-n if n < 0 else 4 + 2 * n + h], axis_nbr[axis])

    both = range(2)
    xy_far1 = [hop(0, h, a_cols((1, 1, 1), h), held(0, h), AX) for h in both]
    xy_near1 = [hop(1, h, a_cols((1, 1, 0), h), held(1, h), AX) for h in both]
    x_far = [hop(2, h, a_cols((1, 0, 1), h), far(4, h), AX) for h in both]
    y_far = [hop(3, h, a_cols((0, 1, 1), h), far(2, h), AY) for h in both]
    xy_far2 = [hop(4, h, held(0, h), far(6, h), AY) for h in both]
    z_own = [hop(-1, h, a_cols((0, 0, 1), h), near(1, h), AZ) for h in both]
    z_y = [hop(-1, h, far(2, h), near(3, h), AZ) for h in both]
    xy_near2 = [hop(-2, h, held(1, h), near(6, h), AY) for h in both]
    z_xy = [hop(-2, h, far(6, h), near(7, h), AZ) for h in both]
    x_near = [hop(-3, h, a_cols((1, 0, 0), h), near(4, h), AX) for h in both]
    y_near = [hop(-3, h, a_cols((0, 1, 0), h), near(2, h), AY) for h in both]
    z_x = [hop(-3, h, far(4, h), near(5, h), AZ) for h in both]
    hops = 24

    def end_group(n, copies):
        wait_bytes(a_v.at[pl.ds(0, copies // 2), :, pl.ds(0, 2 * depth)], ch_recv.at[n])

    own = [pltpu.make_async_copy(a_cols((0, 0, 0), h), near(0, h), own_sem) for h in both]
    own += [pltpu.make_async_copy(a_cols((0, 0, 1), h), far(0, h), own_sem) for h in both]

    def a_chunk(n):
        d, k = (n // 4) * 2, n % 4
        return send(a_v.at[d, :, pl.ds(pl.multiple_of(k * half, half), half)],
                    a_v.at[d + 1, :, pl.ds(pl.multiple_of(2 * depth + k * half, half), half)],
                    ch_send.at[n % RC], ch_recv.at[0], axis_nbr[AZ])

    def b_chunk(q, h):
        rows = pl.ds(pl.multiple_of(h * half, half), half)
        n = 16 + 2 * q + h
        return send(b_hbm.at[rows, their_cols(q)], bz_hbm.at[q, rows], ch_send.at[n % RC], ch_recv.at[1 + q], axis_nbr[AZ])

    def last_chunk():
        return send(b_hbm.at[:, last_cols(1 - z)], bz_hbm.at[paired, :, 0:W], ch_send.at[chunks % RC], ch_recv.at[1 + paired], axis_nbr[AZ])

    def start_chunks(i):
        def body(n, carry):
            when(n, 0, 16, lambda: a_chunk(n).start())
            when(n, 16, chunks, lambda: b_chunk((n - 16) // 2, (n - 16) % 2).start())
            when(n, chunks, chunks + 1, lambda: last_chunk().start())
            return carry

        lax.fori_loop(rate * i // 100 + AHEAD, rate * (i + 1) // 100 + AHEAD, body, 0)

    def end_chunks(i):
        def body(n, carry):
            when(n, 0, 16, lambda: a_chunk(n).wait_send())
            when(n, 16, chunks, lambda: b_chunk((n - 16) // 2, (n - 16) % 2).wait_send())
            when(n, chunks, chunks + 1, lambda: last_chunk().wait_send())
            return carry

        lax.fori_loop(rate * i // 100 + AHEAD, rate * (i + 1) // 100 + AHEAD, body, 0)

    def bx_copy(t):
        return send(b_hbm.at[:, tile_cols(t)], bx_hbm.at[t], bx_send.at[t % RX], bx_recv.at[t % RX], partner)

    def bxz_copy(q):
        return send(bz_hbm.at[q], bxz_hbm.at[q], bxz_send.at[q % RZ], bxz_recv.at[q % RZ], partner)

    def last_bx():
        return send(b_hbm.at[:, last_cols(z)], bx_hbm.at[last, :, 0:W], bx_send.at[last % RX], bx_recv.at[last % RX], partner)

    def last_bxz():
        return send(bz_hbm.at[paired, :, 0:W], bxz_hbm.at[paired, :, 0:W], bxz_send.at[paired % RZ], bxz_recv.at[paired % RZ], partner)

    def last_piece(k):
        src = (b_hbm.at[:, last_cols(z)], bx_hbm.at[last, :, 0:W], bz_hbm.at[paired, :, 0:W], bxz_hbm.at[paired, :, 0:W])[k]
        return pltpu.make_async_copy(src, b_v.at[last % 2, pl.ds(k * depth, depth), 0:W], b_sem.at[last % 2])

    def b_piece(t, k):
        src = (b_hbm.at[:, tile_cols(t)], bx_hbm.at[t], bz_hbm.at[t - plain], bxz_hbm.at[t - plain])[k]
        return pltpu.make_async_copy(src, b_v.at[t % 2, pl.ds(k * depth, depth)], b_sem.at[t % 2])

    def fetch_near(t):
        b_piece(t, 0).start()
        bx_copy(t).wait_recv()
        b_piece(t, 1).start()

    def fetch_far(t):
        wait_bytes(bz_hbm.at[t - plain], ch_recv.at[1 + t - plain])
        bxz_copy(t - plain).start()
        b_piece(t, 2).start()

    def fetch_last(t):
        bxz_copy(t - plain).wait_recv()
        b_piece(t, 3).start()

    def last_near():
        last_piece(0).start()
        last_bx().wait_recv()
        last_piece(1).start()

    def last_far():
        last_chunk().wait_recv()
        last_bxz().start()
        last_piece(2).start()

    def last_fetch():
        last_bxz().wait_recv()
        last_piece(3).start()

    def partial(t, d, k):
        s = t % 2
        dx, dy, dz = bits_of(d)
        part = jnp.dot(a_v[d, :, 0:k * depth], b_v[s, 0:k * depth], preferred_element_type=jnp.float32)
        p_v[s, 0, dx, dy * 2 + dz] = part[:, 0:W]
        p_v[s, 1, dy, dx * 2 + dz] = part[:, W:C]

    def last_partials():
        s = last % 2

        def body(d, carry):
            dx, dy, dz = bits_of(d)
            part = jnp.dot(a_v[d], b_v[s, :, 0:W], preferred_element_type=jnp.float32)
            p_v[s, 0, dx, dy * 2 + dz, 0:upper] = part[0:upper]
            p_v[s, 1, dy, dx * 2 + dz, 0:upper] = part[upper:rows]
            return carry

        lax.fori_loop(0, 8, body, 0)

    def partials(t, k, n=8, order=lambda j: j):
        def body(j, carry):
            partial(t, order(j), k)
            return carry

        lax.fori_loop(0, n, body, 0)

    def first_two(n, order):
        def body(j, carry):
            partial(j // n, order(j % n), 2)
            return carry

        lax.fori_loop(0, 2 * n, body, 0)

    def send1(t, g, k, n=rows):
        s, blocks, part = t % 2, pl.ds(2 * k, 2), pl.ds(0, n)
        return send(p_v.at[s, g, 1, blocks, part], r1_v.at[s, g, blocks, part],
                    s1_sem.at[s, g], r1_sem.at[s, g, k], axis_nbr[g])

    def send2(t, g, k, n=rows):
        s, part = t % 2, pl.ds(0, n)
        return send(s2_v.at[s, g, 2 + k, part], r2_v.at[s, g, k, part],
                    s2_sem.at[s, g], r2_sem.at[s, g, k], axis_nbr[1 - g])

    def sent1(t, g, n=rows):
        wait_bytes(p_v.at[t % 2, g, 1, :, pl.ds(0, n)], s1_sem.at[t % 2, g])

    def sent2(t, g, n=rows):
        wait_bytes(r2_v.at[t % 2, g, :, pl.ds(0, n)], s2_sem.at[t % 2, g])

    def send3(t, g):
        s = t % D3
        return send(s3_v.at[s, g, 1], r3_v.at[s, g], s3_sem.at[s], r3_sem.at[s], axis_nbr[AZ])

    def pair_there(t, g):
        s = t % DO
        return send(q_v.at[s, g], c_v.at[:, tile_cols(t, g)], qs_sem.at[s], qr_sem, axis_nbr[AZ])

    def last_there(g):
        s = last % DO
        return send(q_v.at[s, g, pl.ds(0, upper)], c_v.at[pl.ds(g * upper, upper), last_cols(z)],
                    qs_sem.at[s], qr_sem, axis_nbr[AZ])

    def sent3(t):
        wait_bytes(r3_v.at[t % D3], s3_sem.at[t % D3])

    def got3(t):
        wait_bytes(r3_v.at[t % D3], r3_sem.at[t % D3])

    def pair_sent(t):
        wait_bytes(q_v.at[t % DO], qs_sem.at[t % DO])

    def take(t, g, phase, slots, high):
        when(t, slots, high, lambda: pl.semaphore_wait(credit.at[phase, g], 1))

    def give(t, g, phase, axis, slots, high):
        when(t, 0, high - slots, lambda: pl.semaphore_signal(
            credit.at[phase, g], inc=1, device_id=axis_nbr[axis], device_id_type=MESH))

    for copy in own:
        copy.start()
    pl.semaphore_wait(barrier, 4)
    for group in (xy_far1, y_far, z_own, xy_near1, x_far, x_near):
        for copy in group:
            copy.start()
    for t in range(min(LOOK, tiles)):
        bx_copy(t).start()
    for t in range(2):
        fetch_near(t)
    for h in both:
        y_far[h].wait_recv()
        z_y[h].start()
        xy_far1[h].wait_recv()
        xy_far2[h].start()
    for h in both:
        xy_near1[h].wait_recv()
        xy_near2[h].start()
        xy_far2[h].wait_recv()
        z_xy[h].start()
    for copy in y_near:
        copy.start()
    for t in range(2):
        wait_bytes(b_v.at[t, pl.ds(0, 2 * depth)], b_sem.at[t])
    wait_bytes(a_v.at[0], own_sem)
    end_group(1, 4)
    first_two(3, lambda j: j + j // 2)
    for h in both:
        x_far[h].wait_recv()
        z_x[h].start()
    for n in range(AHEAD):
        a_chunk(n).start()
    end_group(2, 4)
    first_two(2, lambda j: 6 + j)
    for t in range(2):
        for g in both:
            send1(t, g, 1).start()
    end_group(3, 6)

    def last_three(j):
        return 2 + (3 * j + 1) // 2

    def add3(t, g):
        c_v[:, tile_cols(t, g)] = (s3_v[t % D3, g, 0] + r3_v[t % D3, g]).astype(jnp.bfloat16)

    def start_late():
        def body(t, carry):
            for g in both:
                when(t, D3, plain, lambda g=g: pl.semaphore_wait(credit.at[2, g], 1))
                send3(t, g).start()
            return carry

        lax.fori_loop(plain - LATE, plain, body, 0)

    def each(low, high, fn):
        def body(n, carry):
            fn(n)
            return carry

        lax.fori_loop(low, high, body, 0)

    def end_hops():
        wait_bytes(a_v.at[pl.ds(0, hops // 4)], hop_send)
        for n in range(AHEAD):
            a_chunk(n).wait_send()

    def step(i, carry):
        t = i
        when(t, 0, tiles, lambda: start_chunks(t))
        when(t, LAG, tiles + 3, lambda: end_chunks(t - LAG))
        when(t, 1, tiles + 1, lambda: bx_copy(t - 1).wait_send())
        when(t, plain + 1, tiles + 1, lambda: bxz_copy(t - 1 - plain).wait_send())
        when(t, LAG, LAG + 1, end_hops)
        when(t, 0, tiles - LOOK, lambda: bx_copy(t + LOOK).start())
        when(t, tiles - LOOK, tiles - LOOK + 1, lambda: last_bx().start())
        when(t, 1, tiles - 1, lambda: fetch_near(t + 1))
        when(t, tiles - 1, tiles, last_near)
        for g in both:
            when(t, 2, tiles + 2, lambda g=g: sent1(t - 2, g))

        def wait_b(pieces):
            wait_bytes(b_v.at[t % 2, pl.ds(0, pieces * depth)], b_sem.at[t % 2])

        def near_products():
            wait_b(2)
            partials(t, 2)

        def all_products():
            wait_b(4)
            partials(t, 4)

        def last_products():
            wait_bytes(b_v.at[last % 2, :, 0:W], b_sem.at[last % 2])
            last_partials()
            for g in both:
                pl.semaphore_wait(credit.at[0, g], 1)
                send1(last, g, 1, upper).start()
            for g in both:
                send1(last, g, 0, upper).start()

        def wait_far():
            wait_bytes(a_v.at[pl.ds(0, 4), :, pl.ds(2 * depth, 2 * depth)], ch_recv.at[0])

        when(t, 0, 2, lambda: partials(t, 2, 3, last_three))
        when(t, 2, plain, near_products)
        when(t, plain, plain + 1, wait_far)
        when(t, plain, tiles, all_products)
        when(t, last, last + 1, last_products)
        for g in both:
            take(t, g, 0, 2, tiles)
            when(t, 2, tiles, lambda g=g: send1(t, g, 1).start())
        for g in both:
            when(t, 0, tiles, lambda g=g: send1(t, g, 0).start())
        when(t, plain - 1, tiles - 1, lambda: fetch_far(t + 1))
        when(t, tiles - 1, tiles, last_far)

        t1 = i - 1

        def add1(g, k, n=rows):
            s, blocks, part = t1 % 2, pl.ds(2 * k, 2), pl.ds(0, n)
            send1(t1, g, k, n).wait_recv()
            s2_v[s, g, blocks, part] = p_v[s, g, 0, blocks, part] + r1_v[s, g, blocks, part]

        def last1():
            for g in both:
                add1(g, 1, upper)
                pl.semaphore_wait(credit.at[1, g], 1)
                send2(last, g, 1, upper).start()
            for g in both:
                send2(last - 1, g, 0).start()
            for g in both:
                send2(last, g, 0, upper).start()
            for g in both:
                add1(g, 0, upper)

        for g in both:
            when(t1, 2, tiles + 1, lambda g=g: sent2(t1 - 2, g))
            when(t1, 0, tiles, lambda g=g: add1(g, 1))
            take(t1, g, 1, 2, tiles)
            when(t1, 0, tiles, lambda g=g: send2(t1, g, 1).start())
            when(t1, 0, tiles - 1, lambda g=g: send2(t1, g, 0).start())
        for g in both:
            when(t1, 0, tiles, lambda g=g: add1(g, 0))
            give(t1, g, 0, g, 2, last + 1)
        when(t1, last, last + 1, last1)

        t2 = i - 2

        def sum2(t, g, k, n=rows):
            part = pl.ds(0, n)
            send2(t, g, k, n).wait_recv()
            return s2_v[t % 2, g, k, part] + r2_v[t % 2, g, k, part]

        def last2():
            for g in both:
                q_v[last % DO, g, pl.ds(0, upper)] = sum2(last, g, 1, upper).astype(jnp.bfloat16)
                last_there(g).start()
            each(plain - LATE, plain, got3)
            for g in both:
                each(plain - LATE, plain, lambda t: add3(t, g))
            each(plain - LATE, plain, sent3)
            each(tiles + 3 - LAG, tiles, end_chunks)
            each(max(plain, last + 1 - DO), tiles - 1, pair_sent)
            last_bx().wait_send()
            last_bxz().wait_send()
            for g in both:
                sent1(last, g, upper)
            for g in both:
                add2_here(last - 1, g)
            for g in both:
                c_v[pl.ds(g * upper, upper), last_cols(z)] = sum2(last, g, 0, upper).astype(jnp.bfloat16)

        def add2(g, k):
            s3_v[t2 % D3, g, k] = sum2(t2, g, k)

        def add2_there(g):
            q_v[t2 % DO, g] = sum2(t2, g, 1).astype(jnp.bfloat16)

        def add2_here(t, g):
            c_v[:, tile_cols(t, g)] = sum2(t, g, 0).astype(jnp.bfloat16)

        when(t2, D3, plain - LATE + D3, lambda: sent3(t2 - D3))
        when(t2, plain + DO, last + 1, lambda: pair_sent(t2 - DO))
        for g in both:
            when(t2, 0, plain, lambda g=g: add2(g, 1))
            when(t2, plain, tiles, lambda g=g: add2_there(g))
            take(t2, g, 2, D3, plain - LATE)
            when(t2, 0, plain - LATE, lambda g=g: send3(t2, g).start())
            when(t2, plain, tiles, lambda g=g: pair_there(t2, g).start())
        for g in both:
            when(t2, 0, plain, lambda g=g: add2(g, 0))
            when(t2, plain, tiles - 1, lambda g=g: add2_here(t2, g))
            give(t2, g, 1, 1 - g, 2, last + 1)
        when(t2, last, last + 1, last2)

        t3 = i - 1 - D3
        when(t3, 0, plain - LATE, lambda: got3(t3))
        for g in both:
            when(t3, 0, plain - LATE, lambda g=g: add3(t3, g))
            give(t3, g, 2, AZ, D3, plain)
        when(t, last - 1, last, start_late)
        when(t, plain - 1, tiles - 1, lambda: fetch_last(t + 1))
        when(t, tiles - 1, tiles, last_fetch)
        return carry

    lax.fori_loop(0, tiles + 3, step, 0)

    each(max(plain, tiles - 1), tiles, pair_sent)
    for g in both:
        sent2(last - 1, g)
        sent2(last, g, upper)
    wait_bytes(q_v.at[last % DO, :, pl.ds(0, upper)], qs_sem.at[last % DO])
    wait_bytes(c_v.at[:, pl.ds(0, paired * C + W)], qr_sem)


def solution(mesh):
    spec_rows = P(("dp", "tp"), None)

    def local_block(a_rows, b_rows):
        rows, inner = a_rows.shape
        depth, columns = b_rows.shape
        plain, paired = counts(columns)
        tiles = plain + paired
        f32, bf16 = jnp.float32, jnp.bfloat16
        dma = pltpu.SemaphoreType.DMA
        out = pl.pallas_call(
            kernel,
            name="matmul_reduce_scatter",
            out_shape=(
                pltpu.VMEM((rows, columns), bf16),
                jax.ShapeDtypeStruct((tiles + 1, depth, C), bf16),
                jax.ShapeDtypeStruct((paired + 1, depth, C), bf16),
                jax.ShapeDtypeStruct((paired + 1, depth, C), bf16),
                jax.ShapeDtypeStruct((2, rows, 2 * depth), bf16),
            ),
            in_specs=[pl.BlockSpec(memory_space=pl.ANY)] * 2,
            out_specs=(pl.BlockSpec(memory_space=pltpu.VMEM),) + (pl.BlockSpec(memory_space=pl.ANY),) * 4,
            scratch_shapes=[
                pltpu.VMEM((8, rows, 4 * depth), bf16),
                pltpu.VMEM((2, 4 * depth, C), bf16),
                pltpu.VMEM((2, 2, 2, 4, rows, W), f32),
                pltpu.VMEM((2, 2, 4, rows, W), f32),
                pltpu.VMEM((2, 2, 4, rows, W), f32),
                pltpu.VMEM((2, 2, 2, rows, W), f32),
                pltpu.VMEM((D3, 2, 2, rows, W), f32),
                pltpu.VMEM((D3, 2, rows, W), f32),
                pltpu.VMEM((DO, 2, rows, W), bf16),
                dma, dma, dma((RX,)), dma((RX,)), dma((RZ,)), dma((RZ,)), dma((RC,)), dma((max(2 + paired, 14),)), dma((2,)),
                dma((2, 2)), dma((2, 2, 2)), dma((2, 2)), dma((2, 2, 2)), dma((D3,)), dma((D3,)), dma((DO,)), dma,
                pltpu.SemaphoreType.REGULAR((3, 2)),
            ],
            compiler_params=pltpu.CompilerParams(
                collective_id=0, has_side_effects=True, vmem_limit_bytes=56 * 1024 * 1024),
            cost_estimate=pl.CostEstimate(
                flops=2 * 8 * rows * 2 * depth * columns, bytes_accessed=6 * depth * columns, transcendentals=0),
        )(a_rows, b_rows)
        return out[0]

    return jax.shard_map(local_block, mesh=mesh, in_specs=(spec_rows, spec_rows), out_specs=spec_rows, check_vma=False)
```

profile of v0, /device:TPU:0, one launch (start us, length us, event | category | flops | bytes accessed | tf_op | source)
XLA Modules:
  0.0 889.7 jit_solution(6053501736263159708)
XLA Ops:
  0.0 886.6 %matmul_reduce_scatter.1 = (bf16[256,14336]{1,0:T(8,128)(2,1)S(1)}, bf16[42,2048,256]{2,1,0:T(8,128)(2,1)}, bf16[15,2048,256]{2,1,0:T(8,128)(2,1)}, bf16[15,2048,256]{2,1,0:T(8,128)(2,1)}, bf16[2,256,4096]{2,1,0:T(8,128)(2,1)}) custom-call(bf16[256,32768]{1,0:T(8,128)(2,1)} %a_hbm.1, bf16[2048,14336]{1,0:T(8,128)(2,1)} %b_hbm.1), custom_call_target="tpu_custom_call" | custom-call | flops 240518168576 | bytes 176160768 | tf_op jit(solution)/shard_map/matmul_reduce_scatter/pallas_call | solution.py:504
  886.6 3.1 copy.4
where the time goes:
time: 890 us
  Pallas kernels  887 us (100%)
    pallas_call x1, Pallas kernels, local_block(): pl.pallas_call(kernel, name='matmul_reduce_scatter', out_shape=(pltpu.VME...  887 us

commit v1 on v0

--- a/solution.py
+++ b/solution.py
@@ -370,6 +370,8 @@
         def last_products():
             wait_bytes(b_v.at[last % 2, :, 0:W], b_sem.at[last % 2])
             last_partials()
+
+        def start_last():
             for g in both:
                 pl.semaphore_wait(credit.at[0, g], 1)
                 send1(last, g, 1, upper).start()
@@ -417,6 +419,7 @@
             take(t1, g, 1, 2, tiles)
             when(t1, 0, tiles, lambda g=g: send2(t1, g, 1).start())
             when(t1, 0, tiles - 1, lambda g=g: send2(t1, g, 0).start())
+        when(t, last, last + 1, start_last)
         for g in both:
             when(t1, 0, tiles, lambda g=g: add1(g, 0))
             give(t1, g, 0, g, 2, last + 1)

time: 890 us -> 890 us (level)
  no operation moved by 1% of the time
where the time goes in v1:
time: 890 us
  Pallas kernels  887 us (100%)
    pallas_call x1, Pallas kernels, local_block(): pl.pallas_call(kernel, name='matmul_reduce_scatter', out_shape=(pltpu.VME...  887 us

profile of v1, /device:TPU:0, one launch (start us, length us, event | category | flops | bytes accessed | tf_op | source)
XLA Modules:
  0.0 889.7 jit_solution(2898140167749676586)
XLA Ops:
  0.0 886.6 %matmul_reduce_scatter.1 = (bf16[256,14336]{1,0:T(8,128)(2,1)S(1)}, bf16[42,2048,256]{2,1,0:T(8,128)(2,1)}, bf16[15,2048,256]{2,1,0:T(8,128)(2,1)}, bf16[15,2048,256]{2,1,0:T(8,128)(2,1)}, bf16[2,256,4096]{2,1,0:T(8,128)(2,1)}) custom-call(bf16[256,32768]{1,0:T(8,128)(2,1)} %a_hbm.1, bf16[2048,14336]{1,0:T(8,128)(2,1)} %b_hbm.1), custom_call_target="tpu_custom_call" | custom-call | flops 240518168576 | bytes 176160768 | tf_op jit(solution)/shard_map/matmul_reduce_scatter/pallas_call | solution.py:507
  886.6 3.1 copy.4

commit v2 on v1

--- a/solution.py
+++ b/solution.py
@@ -396,32 +396,30 @@
 
         t1 = i - 1
 
-        def add1(g, k, n=rows):
-            s, blocks, part = t1 % 2, pl.ds(2 * k, 2), pl.ds(0, n)
-            send1(t1, g, k, n).wait_recv()
+        def add1(t, g, k, n=rows):
+            s, blocks, part = t % 2, pl.ds(2 * k, 2), pl.ds(0, n)
+            send1(t, g, k, n).wait_recv()
             s2_v[s, g, blocks, part] = p_v[s, g, 0, blocks, part] + r1_v[s, g, blocks, part]
 
         def last1():
             for g in both:
-                add1(g, 1, upper)
+                add1(last, g, 1, upper)
                 pl.semaphore_wait(credit.at[1, g], 1)
                 send2(last, g, 1, upper).start()
             for g in both:
                 send2(last - 1, g, 0).start()
             for g in both:
                 send2(last, g, 0, upper).start()
-            for g in both:
-                add1(g, 0, upper)
 
         for g in both:
             when(t1, 2, tiles + 1, lambda g=g: sent2(t1 - 2, g))
-            when(t1, 0, tiles, lambda g=g: add1(g, 1))
+            when(t1, 0, tiles, lambda g=g: add1(t1, g, 1))
             take(t1, g, 1, 2, tiles)
             when(t1, 0, tiles, lambda g=g: send2(t1, g, 1).start())
             when(t1, 0, tiles - 1, lambda g=g: send2(t1, g, 0).start())
         when(t, last, last + 1, start_last)
         for g in both:
-            when(t1, 0, tiles, lambda g=g: add1(g, 0))
+            when(t1, 0, tiles, lambda g=g: add1(t1, g, 0))
             give(t1, g, 0, g, 2, last + 1)
         when(t1, last, last + 1, last1)
 
@@ -433,6 +431,8 @@
             return s2_v[t % 2, g, k, part] + r2_v[t % 2, g, k, part]
 
         def last2():
+            for g in both:
+                add1(last, g, 0, upper)
             for g in both:
                 q_v[last % DO, g, pl.ds(0, upper)] = sum2(last, g, 1, upper).astype(jnp.bfloat16)
                 last_there(g).start()

time: 890 us -> 890 us (level)
  no operation moved by 1% of the time
where the time goes in v2:
time: 890 us
  Pallas kernels  887 us (100%)
    pallas_call x1, Pallas kernels, local_block(): pl.pallas_call(kernel, name='matmul_reduce_scatter', out_shape=(pltpu.VME...  887 us

profile of v2, /device:TPU:0, one launch (start us, length us, event | category | flops | bytes accessed | tf_op | source)
XLA Modules:
  0.0 889.7 jit_solution(16092659662008137648)
XLA Ops:
  0.0 886.6 %matmul_reduce_scatter.1 = (bf16[256,14336]{1,0:T(8,128)(2,1)S(1)}, bf16[42,2048,256]{2,1,0:T(8,128)(2,1)}, bf16[15,2048,256]{2,1,0:T(8,128)(2,1)}, bf16[15,2048,256]{2,1,0:T(8,128)(2,1)}, bf16[2,256,4096]{2,1,0:T(8,128)(2,1)}) custom-call(bf16[256,32768]{1,0:T(8,128)(2,1)} %a_hbm.1, bf16[2048,14336]{1,0:T(8,128)(2,1)} %b_hbm.1), custom_call_target="tpu_custom_call" | custom-call | flops 240518168576 | bytes 176160768 | tf_op jit(solution)/shard_map/matmul_reduce_scatter/pallas_call | solution.py:507
  886.6 3.1 copy.4

commit v3 on v2

--- a/solution.py
+++ b/solution.py
@@ -479,7 +479,7 @@
         for g in both:
             when(t3, 0, plain - LATE, lambda g=g: add3(t3, g))
             give(t3, g, 2, AZ, D3, plain)
-        when(t, last - 1, last, start_late)
+        when(t, last - 2, last - 1, start_late)
         when(t, plain - 1, tiles - 1, lambda: fetch_last(t + 1))
         when(t, tiles - 1, tiles, last_fetch)
         return carry

time: 890 us -> 889 us (level)
  no operation moved by 1% of the time
where the time goes in v3:
time: 889 us
  Pallas kernels  886 us (100%)
    pallas_call x1, Pallas kernels, local_block(): pl.pallas_call(kernel, name='matmul_reduce_scatter', out_shape=(pltpu.VME...  886 us

profile of v3, /device:TPU:0, one launch (start us, length us, event | category | flops | bytes accessed | tf_op | source)
XLA Modules:
  0.0 888.9 jit_solution(14257781452299867621)
XLA Ops:
  0.0 885.9 %matmul_reduce_scatter.1 = (bf16[256,14336]{1,0:T(8,128)(2,1)S(1)}, bf16[42,2048,256]{2,1,0:T(8,128)(2,1)}, bf16[15,2048,256]{2,1,0:T(8,128)(2,1)}, bf16[15,2048,256]{2,1,0:T(8,128)(2,1)}, bf16[2,256,4096]{2,1,0:T(8,128)(2,1)}) custom-call(bf16[256,32768]{1,0:T(8,128)(2,1)} %a_hbm.1, bf16[2048,14336]{1,0:T(8,128)(2,1)} %b_hbm.1), custom_call_target="tpu_custom_call" | custom-call | flops 240518168576 | bytes 176160768 | tf_op jit(solution)/shard_map/matmul_reduce_scatter/pallas_call | solution.py:507
  885.9 3.1 copy.4

commit v4 on v3

--- a/solution.py
+++ b/solution.py
@@ -279,7 +279,10 @@
     for copy in own:
         copy.start()
     pl.semaphore_wait(barrier, 4)
-    for group in (xy_far1, y_far, z_own, xy_near1, x_far, x_near):
+    for h in both:
+        for group in (xy_far1, y_far, z_own):
+            group[h].start()
+    for group in (xy_near1, x_far, x_near):
         for copy in group:
             copy.start()
     for t in range(min(LOOK, tiles)):
@@ -492,6 +495,15 @@
         sent2(last, g, upper)
     wait_bytes(q_v.at[last % DO, :, pl.ds(0, upper)], qs_sem.at[last % DO])
     wait_bytes(c_v.at[:, pl.ds(0, paired * C + W)], qr_sem)
+
+
+def write_out(c_v, c_hbm, sem):
+    rows = c_v.shape[0] // 8
+    copies = [pltpu.make_async_copy(c_v.at[pl.ds(i * rows, rows)], c_hbm.at[pl.ds(i * rows, rows)], sem.at[i]) for i in range(8)]
+    for copy in copies:
+        copy.start()
+    for copy in copies:
+        copy.wait()
 
 
 def solution(mesh):
@@ -535,6 +547,15 @@
             cost_estimate=pl.CostEstimate(
                 flops=2 * 8 * rows * 2 * depth * columns, bytes_accessed=6 * depth * columns, transcendentals=0),
         )(a_rows, b_rows)
-        return out[0]
+        return pl.pallas_call(
+            write_out,
+            name="write_out",
+            out_shape=jax.ShapeDtypeStruct((rows, columns), bf16),
+            in_specs=[pl.BlockSpec(memory_space=pltpu.VMEM)],
+            out_specs=pl.BlockSpec(memory_space=pl.ANY),
+            scratch_shapes=[dma((8,))],
+            compiler_params=pltpu.CompilerParams(vmem_limit_bytes=1024 * 1024),
+            cost_estimate=pl.CostEstimate(flops=0, bytes_accessed=4 * rows * columns, transcendentals=0),
+        )(out[0])
 
     return jax.shard_map(local_block, mesh=mesh, in_specs=(spec_rows, spec_rows), out_specs=spec_rows, check_vma=False)

time: 889 us -> 889 us (level)
  no operation moved by 1% of the time
where the time goes in v4:
time: 889 us
  Pallas kernels  889 us (100%)
    pallas_call x1, Pallas kernels, local_block(): pl.pallas_call(kernel, name='matmul_reduce_scatter', out_shape=(pltpu.VME...  886 us

profile of v4, /device:TPU:0, one launch (start us, length us, event | category | flops | bytes accessed | tf_op | source)
XLA Modules:
  0.0 888.9 jit_solution(13891222788851980608)
XLA Ops:
  0.0 885.9 %matmul_reduce_scatter.1 = (bf16[256,14336]{1,0:T(8,128)(2,1)S(1)}, bf16[42,2048,256]{2,1,0:T(8,128)(2,1)}, bf16[15,2048,256]{2,1,0:T(8,128)(2,1)}, bf16[15,2048,256]{2,1,0:T(8,128)(2,1)}, bf16[2,256,4096]{2,1,0:T(8,128)(2,1)}) custom-call(bf16[256,32768]{1,0:T(8,128)(2,1)} %a_hbm.1, bf16[2048,14336]{1,0:T(8,128)(2,1)} %b_hbm.1), custom_call_target="tpu_custom_call" | custom-call | flops 240518168576 | bytes 176160768 | tf_op jit(solution)/shard_map/matmul_reduce_scatter/pallas_call | solution.py:519
  885.9 3.1 write_out.1

commit v5 on v3

--- a/solution.py
+++ b/solution.py
@@ -30,7 +30,7 @@
 def kernel(a_hbm, b_hbm, c_v, bx_hbm, bz_hbm, bxz_hbm, relay,
            a_v, b_v, p_v, r1_v, s2_v, r2_v, s3_v, r3_v, q_v,
            hop_send, own_sem, bx_send, bx_recv, bxz_send, bxz_recv, ch_send, ch_recv, b_sem,
-           s1_sem, r1_sem, s2_sem, r2_sem, s3_sem, r3_sem, qs_sem, qr_sem, credit):
+           s1_sem, r1_sem, rk_sem, s2_sem, r2_sem, s3_sem, r3_sem, qs_sem, qr_sem, credit):
     depth, columns = b_hbm.shape
     plain, paired = counts(columns)
     tiles = plain + paired
@@ -231,21 +231,42 @@
 
         lax.fori_loop(0, 2 * n, body, 0)
 
-    def send1(t, g, k, n=rows):
-        s, blocks, part = t % 2, pl.ds(2 * k, 2), pl.ds(0, n)
-        return send(p_v.at[s, g, 1, blocks, part], r1_v.at[s, g, blocks, part],
-                    s1_sem.at[s, g], r1_sem.at[s, g, k], axis_nbr[g])
+    def send1(t, g, k):
+        s, blocks = t % 2, pl.ds(2 * k, 2)
+        return send(p_v.at[s, g, 1, blocks], r1_v.at[s, g, blocks], s1_sem.at[s], r1_sem.at[s, k], axis_nbr[g])
+
+    def got1(t, k):
+        wait_bytes(r1_v.at[t % 2, :, pl.ds(2 * k, 2)], r1_sem.at[t % 2, k])
+
+    def sent1(t):
+        wait_bytes(r1_v.at[t % 2], s1_sem.at[t % 2])
 
     def send2(t, g, k, n=rows):
         s, part = t % 2, pl.ds(0, n)
-        return send(s2_v.at[s, g, 2 + k, part], r2_v.at[s, g, k, part],
-                    s2_sem.at[s, g], r2_sem.at[s, g, k], axis_nbr[1 - g])
-
-    def sent1(t, g, n=rows):
-        wait_bytes(p_v.at[t % 2, g, 1, :, pl.ds(0, n)], s1_sem.at[t % 2, g])
-
-    def sent2(t, g, n=rows):
-        wait_bytes(r2_v.at[t % 2, g, :, pl.ds(0, n)], s2_sem.at[t % 2, g])
+        return send(s2_v.at[s, g, 2 + k, part], r2_v.at[s, g, k, part], s2_sem.at[s], r2_sem.at[s, k], axis_nbr[1 - g])
+
+    def got2(t, k, n=rows):
+        wait_bytes(r2_v.at[t % 2, :, k, pl.ds(0, n)], r2_sem.at[t % 2, k])
+
+    def sent2(t, n=rows):
+        wait_bytes(r2_v.at[t % 2, :, :, pl.ds(0, n)], s2_sem.at[t % 2])
+
+    pieces = (pl.ds(2, 2), pl.ds(1, 1), pl.ds(0, 1))
+    last_part = pl.ds(0, upper)
+
+    def last_sem(k):
+        return (r1_sem.at[last % 2, 1], rk_sem, r1_sem.at[last % 2, 0])[k]
+
+    def last_send1(g, k):
+        s = last % 2
+        return send(p_v.at[s, g, 1, pieces[k], last_part], r1_v.at[s, g, pieces[k], last_part],
+                    s1_sem.at[s], last_sem(k), axis_nbr[g])
+
+    def last_add1(k):
+        s = last % 2
+        wait_bytes(r1_v.at[s, :, pieces[k], last_part], last_sem(k))
+        for g in both:
+            s2_v[s, g, pieces[k], last_part] = p_v[s, g, 0, pieces[k], last_part] + r1_v[s, g, pieces[k], last_part]
 
     def send3(t, g):
         s = t % D3
@@ -353,8 +374,7 @@
         when(t, tiles - LOOK, tiles - LOOK + 1, lambda: last_bx().start())
         when(t, 1, tiles - 1, lambda: fetch_near(t + 1))
         when(t, tiles - 1, tiles, last_near)
-        for g in both:
-            when(t, 2, tiles + 2, lambda g=g: sent1(t - 2, g))
+        when(t, 2, tiles + 2, lambda: sent1(t - 2))
 
         def wait_b(pieces):
             wait_bytes(b_v.at[t % 2, pl.ds(0, pieces * depth)], b_sem.at[t % 2])
@@ -371,12 +391,13 @@
             wait_bytes(b_v.at[last % 2, :, 0:W], b_sem.at[last % 2])
             last_partials()
 
-        def start_last():
             for g in both:
                 pl.semaphore_wait(credit.at[0, g], 1)
-                send1(last, g, 1, upper).start()
-            for g in both:
-                send1(last, g, 0, upper).start()
+                last_send1(g, 0).start()
+
+        def start_kept():
+            for g in both:
+                last_send1(g, 1).start()
 
         def wait_far():
             wait_bytes(a_v.at[pl.ds(0, 4), :, pl.ds(2 * depth, 2 * depth)], ch_recv.at[0])
@@ -396,30 +417,33 @@
 
         t1 = i - 1
 
-        def add1(t, g, k, n=rows):
-            s, blocks, part = t % 2, pl.ds(2 * k, 2), pl.ds(0, n)
-            send1(t, g, k, n).wait_recv()
-            s2_v[s, g, blocks, part] = p_v[s, g, 0, blocks, part] + r1_v[s, g, blocks, part]
+        def add1(k):
+            s, blocks = t1 % 2, pl.ds(2 * k, 2)
+            got1(t1, k)
+            for g in both:
+                s2_v[s, g, blocks] = p_v[s, g, 0, blocks] + r1_v[s, g, blocks]
 
         def last1():
-            for g in both:
-                add1(last, g, 1, upper)
+            last_add1(0)
+            for g in both:
                 pl.semaphore_wait(credit.at[1, g], 1)
                 send2(last, g, 1, upper).start()
             for g in both:
                 send2(last - 1, g, 0).start()
             for g in both:
+                last_send1(g, 2).start()
+            for g in both:
                 send2(last, g, 0, upper).start()
 
-        for g in both:
-            when(t1, 2, tiles + 1, lambda g=g: sent2(t1 - 2, g))
-            when(t1, 0, tiles, lambda g=g: add1(t1, g, 1))
+        when(t1, 2, tiles + 1, lambda: sent2(t1 - 2))
+        when(t1, 0, tiles, lambda: add1(1))
+        for g in both:
             take(t1, g, 1, 2, tiles)
             when(t1, 0, tiles, lambda g=g: send2(t1, g, 1).start())
             when(t1, 0, tiles - 1, lambda g=g: send2(t1, g, 0).start())
-        when(t, last, last + 1, start_last)
-        for g in both:
-            when(t1, 0, tiles, lambda g=g: add1(t1, g, 0))
+        when(t, last, last + 1, start_kept)
+        when(t1, 0, tiles, lambda: add1(0))
+        for g in both:
             give(t1, g, 0, g, 2, last + 1)
         when(t1, last, last + 1, last1)
 
@@ -427,14 +451,13 @@
 
         def sum2(t, g, k, n=rows):
             part = pl.ds(0, n)
-            send2(t, g, k, n).wait_recv()
             return s2_v[t % 2, g, k, part] + r2_v[t % 2, g, k, part]
 
         def last2():
-            for g in both:
-                add1(last, g, 0, upper)
-            for g in both:
-                q_v[last % DO, g, pl.ds(0, upper)] = sum2(last, g, 1, upper).astype(jnp.bfloat16)
+            last_add1(1)
+            got2(last, 1, upper)
+            for g in both:
+                q_v[last % DO, g, last_part] = sum2(last, g, 1, upper).astype(jnp.bfloat16)
                 last_there(g).start()
             each(plain - LATE, plain, got3)
             for g in both:
@@ -444,33 +467,38 @@
             each(max(plain, last + 1 - DO), tiles - 1, pair_sent)
             last_bx().wait_send()
             last_bxz().wait_send()
-            for g in both:
-                sent1(last, g, upper)
-            for g in both:
-                add2_here(last - 1, g)
+            add2_here(last - 1)
+            last_add1(2)
+            got2(last, 0, upper)
             for g in both:
                 c_v[pl.ds(g * upper, upper), last_cols(z)] = sum2(last, g, 0, upper).astype(jnp.bfloat16)
 
-        def add2(g, k):
-            s3_v[t2 % D3, g, k] = sum2(t2, g, k)
-
-        def add2_there(g):
-            q_v[t2 % DO, g] = sum2(t2, g, 1).astype(jnp.bfloat16)
-
-        def add2_here(t, g):
-            c_v[:, tile_cols(t, g)] = sum2(t, g, 0).astype(jnp.bfloat16)
+        def add2(k):
+            got2(t2, k)
+            for g in both:
+                s3_v[t2 % D3, g, k] = sum2(t2, g, k)
+
+        def add2_there():
+            got2(t2, 1)
+            for g in both:
+                q_v[t2 % DO, g] = sum2(t2, g, 1).astype(jnp.bfloat16)
+
+        def add2_here(t):
+            got2(t, 0)
+            for g in both:
+                c_v[:, tile_cols(t, g)] = sum2(t, g, 0).astype(jnp.bfloat16)
 
         when(t2, D3, plain - LATE + D3, lambda: sent3(t2 - D3))
         when(t2, plain + DO, last + 1, lambda: pair_sent(t2 - DO))
-        for g in both:
-            when(t2, 0, plain, lambda g=g: add2(g, 1))
-            when(t2, plain, tiles, lambda g=g: add2_there(g))
+        when(t2, 0, plain, lambda: add2(1))
+        when(t2, plain, tiles, add2_there)
+        for g in both:
             take(t2, g, 2, D3, plain - LATE)
             when(t2, 0, plain - LATE, lambda g=g: send3(t2, g).start())
             when(t2, plain, tiles, lambda g=g: pair_there(t2, g).start())
-        for g in both:
-            when(t2, 0, plain, lambda g=g: add2(g, 0))
-            when(t2, plain, tiles - 1, lambda g=g: add2_here(t2, g))
+        when(t2, 0, plain, lambda: add2(0))
+        when(t2, plain, tiles - 1, lambda: add2_here(t2))
+        for g in both:
             give(t2, g, 1, 1 - g, 2, last + 1)
         when(t2, last, last + 1, last2)
 
@@ -487,9 +515,9 @@
     lax.fori_loop(0, tiles + 3, step, 0)
 
     each(max(plain, tiles - 1), tiles, pair_sent)
-    for g in both:
-        sent2(last - 1, g)
-        sent2(last, g, upper)
+    wait_bytes(r1_v.at[last % 2, :, :, last_part], s1_sem.at[last % 2])
+    sent2(last - 1)
+    sent2(last, upper)
     wait_bytes(q_v.at[last % DO, :, pl.ds(0, upper)], qs_sem.at[last % DO])
     wait_bytes(c_v.at[:, pl.ds(0, paired * C + W)], qr_sem)
 
@@ -527,7 +555,7 @@
                 pltpu.VMEM((D3, 2, rows, W), f32),
                 pltpu.VMEM((DO, 2, rows, W), bf16),
                 dma, dma, dma((RX,)), dma((RX,)), dma((RZ,)), dma((RZ,)), dma((RC,)), dma((max(2 + paired, 14),)), dma((2,)),
-                dma((2, 2)), dma((2, 2, 2)), dma((2, 2)), dma((2, 2, 2)), dma((D3,)), dma((D3,)), dma((DO,)), dma,
+                dma((2,)), dma((2, 2)), dma, dma((2,)), dma((2, 2)), dma((D3,)), dma((D3,)), dma((DO,)), dma,
                 pltpu.SemaphoreType.REGULAR((3, 2)),
             ],
             compiler_params=pltpu.CompilerParams(

time: 889 us -> 888 us (level)
  no operation moved by 1% of the time
where the time goes in v5:
time: 888 us
  Pallas kernels  885 us (100%)
    pallas_call x1, Pallas kernels, local_block(): pl.pallas_call(kernel, name='matmul_reduce_scatter', out_shape=(pltpu.VME...  885 us

profile of v5, /device:TPU:0, one launch (start us, length us, event | category | flops | bytes accessed | tf_op | source)
XLA Modules:
  0.0 888.2 jit_solution(3905851450041311703)
XLA Ops:
  0.0 885.2 %matmul_reduce_scatter.1 = (bf16[256,14336]{1,0:T(8,128)(2,1)S(1)}, bf16[42,2048,256]{2,1,0:T(8,128)(2,1)}, bf16[15,2048,256]{2,1,0:T(8,128)(2,1)}, bf16[15,2048,256]{2,1,0:T(8,128)(2,1)}, bf16[2,256,4096]{2,1,0:T(8,128)(2,1)}) custom-call(bf16[256,32768]{1,0:T(8,128)(2,1)} %a_hbm.1, bf16[2048,14336]{1,0:T(8,128)(2,1)} %b_hbm.1), custom_call_target="tpu_custom_call" | custom-call | flops 240518168576 | bytes 176160768 | tf_op jit(solution)/shard_map/matmul_reduce_scatter/pallas_call | solution.py:535
  885.2 3.1 copy.4

commit v6 on v5

--- a/solution.py
+++ b/solution.py
@@ -28,8 +28,8 @@
 
 
 def kernel(a_hbm, b_hbm, c_v, bx_hbm, bz_hbm, bxz_hbm, relay,
-           a_v, b_v, p_v, r1_v, s2_v, r2_v, s3_v, r3_v, q_v,
-           hop_send, own_sem, bx_send, bx_recv, bxz_send, bxz_recv, ch_send, ch_recv, b_sem,
+           head_v, a_v, b_v, p_v, r1_v, s2_v, r2_v, s3_v, r3_v, q_v,
+           head_sem, hop_send, own_sem, bx_send, bx_recv, bxz_send, bxz_recv, ch_send, ch_recv, b_sem,
            s1_sem, r1_sem, rk_sem, s2_sem, r2_sem, s3_sem, r3_sem, qs_sem, qr_sem, credit):
     depth, columns = b_hbm.shape
     plain, paired = counts(columns)
@@ -103,7 +103,7 @@
     x_far = [hop(2, h, a_cols((1, 0, 1), h), far(4, h), AX) for h in both]
     y_far = [hop(3, h, a_cols((0, 1, 1), h), far(2, h), AY) for h in both]
     xy_far2 = [hop(4, h, held(0, h), far(6, h), AY) for h in both]
-    z_own = [hop(-1, h, a_cols((0, 0, 1), h), near(1, h), AZ) for h in both]
+    z_own = hop(-1, 1, a_cols((0, 0, 1), 1), near(1, 1), AZ)
     z_y = [hop(-1, h, far(2, h), near(3, h), AZ) for h in both]
     xy_near2 = [hop(-2, h, held(1, h), near(6, h), AY) for h in both]
     z_xy = [hop(-2, h, far(6, h), near(7, h), AZ) for h in both]
@@ -112,6 +112,13 @@
     z_x = [hop(-3, h, far(4, h), near(5, h), AZ) for h in both]
     hops = 24
 
+    head = rows // 8
+    openers = ((0, a_cols((1, 1, 1), 0), held(0, 0), AX), (3, a_cols((0, 1, 1), 0), far(2, 0), AY),
+               (-1, a_cols((0, 0, 1), 0), near(1, 0), AZ))
+    loads = [pltpu.make_async_copy(src.at[pl.ds(0, head)], head_v.at[i], head_sem) for i, (_, src, _, _) in enumerate(openers)]
+    heads = [hop(n, 0, head_v.at[i], dst.at[pl.ds(0, head)], axis) for i, (n, _, dst, axis) in enumerate(openers)]
+    tails = [hop(n, 0, src.at[pl.ds(head, rows - head)], dst.at[pl.ds(head, rows - head)], axis) for n, src, dst, axis in openers]
+
     def end_group(n, copies):
         wait_bytes(a_v.at[pl.ds(0, copies // 2), :, pl.ds(0, 2 * depth)], ch_recv.at[n])
 
@@ -297,12 +304,16 @@
         when(t, 0, high - slots, lambda: pl.semaphore_signal(
             credit.at[phase, g], inc=1, device_id=axis_nbr[axis], device_id_type=MESH))
 
+    for copy in loads:
+        copy.start()
+    pl.semaphore_wait(barrier, 4)
+    wait_bytes(head_v, head_sem)
+    for copy in heads + tails:
+        copy.start()
+    for copy in (xy_far1[1], y_far[1], z_own, *xy_near1, *x_far, *x_near):
+        copy.start()
     for copy in own:
         copy.start()
-    pl.semaphore_wait(barrier, 4)
-    for group in (xy_far1, y_far, z_own, xy_near1, x_far, x_near):
-        for copy in group:
-            copy.start()
     for t in range(min(LOOK, tiles)):
         bx_copy(t).start()
     for t in range(2):
@@ -545,6 +556,7 @@
             in_specs=[pl.BlockSpec(memory_space=pl.ANY)] * 2,
             out_specs=(pl.BlockSpec(memory_space=pltpu.VMEM),) + (pl.BlockSpec(memory_space=pl.ANY),) * 4,
             scratch_shapes=[
+                pltpu.VMEM((3, rows // 8, depth), bf16),
                 pltpu.VMEM((8, rows, 4 * depth), bf16),
                 pltpu.VMEM((2, 4 * depth, C), bf16),
                 pltpu.VMEM((2, 2, 2, 4, rows, W), f32),
@@ -554,7 +566,7 @@
                 pltpu.VMEM((D3, 2, 2, rows, W), f32),
                 pltpu.VMEM((D3, 2, rows, W), f32),
                 pltpu.VMEM((DO, 2, rows, W), bf16),
-                dma, dma, dma((RX,)), dma((RX,)), dma((RZ,)), dma((RZ,)), dma((RC,)), dma((max(2 + paired, 14),)), dma((2,)),
+                dma, dma, dma, dma((RX,)), dma((RX,)), dma((RZ,)), dma((RZ,)), dma((RC,)), dma((max(2 + paired, 14),)), dma((2,)),
                 dma((2,)), dma((2, 2)), dma, dma((2,)), dma((2, 2)), dma((D3,)), dma((D3,)), dma((DO,)), dma,
                 pltpu.SemaphoreType.REGULAR((3, 2)),
             ],

time: 888 us -> 888 us (level)
  no operation moved by 1% of the time
where the time goes in v6:
time: 888 us
  Pallas kernels  885 us (100%)
    pallas_call x1, Pallas kernels, local_block(): pl.pallas_call(kernel, name='matmul_reduce_scatter', out_shape=(pltpu.VME...  885 us

profile of v6, /device:TPU:0, one launch (start us, length us, event | category | flops | bytes accessed | tf_op | source)
XLA Modules:
  0.0 888.2 jit_solution(11490966417402766653)
XLA Ops:
  0.0 885.2 %matmul_reduce_scatter.1 = (bf16[256,14336]{1,0:T(8,128)(2,1)S(1)}, bf16[42,2048,256]{2,1,0:T(8,128)(2,1)}, bf16[15,2048,256]{2,1,0:T(8,128)(2,1)}, bf16[15,2048,256]{2,1,0:T(8,128)(2,1)}, bf16[2,256,4096]{2,1,0:T(8,128)(2,1)}) custom-call(bf16[256,32768]{1,0:T(8,128)(2,1)} %a_hbm.1, bf16[2048,14336]{1,0:T(8,128)(2,1)} %b_hbm.1), custom_call_target="tpu_custom_call" | custom-call | flops 240518168576 | bytes 176160768 | tf_op jit(solution)/shard_map/matmul_reduce_scatter/pallas_call | solution.py:546
  885.2 3.1 copy.4

commit v7 on v5

--- a/solution.py
+++ b/solution.py
@@ -10,11 +10,11 @@
 C = 2 * W
 LOOK = 2
 D3 = 6
-DO = 6
+DO = 5
 LATE = 4
 AHEAD = 2
 LAG = 5
-RX, RZ, RC = 2 * LOOK, LOOK + 1, 8
+RX, RZ = 2 * LOOK - 1, LOOK
 AX, AY, AZ = 0, 1, 2
 
 
@@ -27,10 +27,15 @@
     return columns // C - 2 * paired - 1, paired
 
 
+def pace(columns):
+    plain, paired = counts(columns)
+    return max(114, -(-1600 // plain), -(-100 * (15 + 2 * paired) // (plain + paired - 1)))
+
+
 def kernel(a_hbm, b_hbm, c_v, bx_hbm, bz_hbm, bxz_hbm, relay,
            a_v, b_v, p_v, r1_v, s2_v, r2_v, s3_v, r3_v, q_v,
-           hop_send, own_sem, bx_send, bx_recv, bxz_send, bxz_recv, ch_send, ch_recv, b_sem,
-           s1_sem, r1_sem, rk_sem, s2_sem, r2_sem, s3_sem, r3_sem, qs_sem, qr_sem, credit):
+            bx_send, bx_recv, bxz_send, bxz_recv, ch_send, ch_recv, b_sem,
+           s1_sem, r1_sem, s2_sem, r2_sem, s3_sem, r3_sem, qs_sem, qr_sem, credit):
     depth, columns = b_hbm.shape
     plain, paired = counts(columns)
     tiles = plain + paired
@@ -38,7 +43,8 @@
     half = depth // 2
     chunks = 16 + 2 * paired
     last = plain + paired
-    rate = max(114, -(-1600 // plain), -(-100 * (15 + 2 * paired) // (tiles - 1)))
+    rate = pace(columns)
+    ring = 5 * rate // 100 + 2
 
     dp, tp = lax.axis_index("dp"), lax.axis_index("tp")
     core, x, y, z = dp % 2, (dp // 2) % 2, dp // 4, tp
@@ -95,7 +101,7 @@
         return relay.at[i, :, pl.ds(h * depth, depth)]
 
     def hop(n, h, src, dst, axis):
-        return send(src, dst, hop_send, ch_recv.at[-n if n < 0 else 4 + 2 * n + h], axis_nbr[axis])
+        return send(src, dst, qr_sem, ch_recv.at[-n if n < 0 else 4 + 2 * n + h], axis_nbr[axis])
 
     both = range(2)
     xy_far1 = [hop(0, h, a_cols((1, 1, 1), h), held(0, h), AX) for h in both]
@@ -115,22 +121,22 @@
     def end_group(n, copies):
         wait_bytes(a_v.at[pl.ds(0, copies // 2), :, pl.ds(0, 2 * depth)], ch_recv.at[n])
 
-    own = [pltpu.make_async_copy(a_cols((0, 0, 0), h), near(0, h), own_sem) for h in both]
-    own += [pltpu.make_async_copy(a_cols((0, 0, 1), h), far(0, h), own_sem) for h in both]
+    own = [pltpu.make_async_copy(a_cols((0, 0, 0), h), near(0, h), ch_recv.at[14]) for h in both]
+    own += [pltpu.make_async_copy(a_cols((0, 0, 1), h), far(0, h), ch_recv.at[14]) for h in both]
 
     def a_chunk(n):
         d, k = (n // 4) * 2, n % 4
         return send(a_v.at[d, :, pl.ds(pl.multiple_of(k * half, half), half)],
                     a_v.at[d + 1, :, pl.ds(pl.multiple_of(2 * depth + k * half, half), half)],
-                    ch_send.at[n % RC], ch_recv.at[0], axis_nbr[AZ])
+                    ch_send.at[n % ring], ch_recv.at[0], axis_nbr[AZ])
 
     def b_chunk(q, h):
         rows = pl.ds(pl.multiple_of(h * half, half), half)
         n = 16 + 2 * q + h
-        return send(b_hbm.at[rows, their_cols(q)], bz_hbm.at[q, rows], ch_send.at[n % RC], ch_recv.at[1 + q], axis_nbr[AZ])
+        return send(b_hbm.at[rows, their_cols(q)], bz_hbm.at[q, rows], ch_send.at[n % ring], ch_recv.at[1 + q], axis_nbr[AZ])
 
     def last_chunk():
-        return send(b_hbm.at[:, last_cols(1 - z)], bz_hbm.at[paired, :, 0:W], ch_send.at[chunks % RC], ch_recv.at[1 + paired], axis_nbr[AZ])
+        return send(b_hbm.at[:, last_cols(1 - z)], bz_hbm.at[paired, :, 0:W], ch_send.at[chunks % ring], ch_recv.at[1 + paired], axis_nbr[AZ])
 
     def start_chunks(i):
         def body(n, carry):
@@ -151,16 +157,16 @@
         lax.fori_loop(rate * i // 100 + AHEAD, rate * (i + 1) // 100 + AHEAD, body, 0)
 
     def bx_copy(t):
-        return send(b_hbm.at[:, tile_cols(t)], bx_hbm.at[t], bx_send.at[t % RX], bx_recv.at[t % RX], partner)
+        return send(b_hbm.at[:, tile_cols(t)], bx_hbm.at[t], bx_send.at[t % 2], bx_recv.at[t % RX], partner)
 
     def bxz_copy(q):
-        return send(bz_hbm.at[q], bxz_hbm.at[q], bxz_send.at[q % RZ], bxz_recv.at[q % RZ], partner)
+        return send(bz_hbm.at[q], bxz_hbm.at[q], bxz_send, bxz_recv.at[q % RZ], partner)
 
     def last_bx():
-        return send(b_hbm.at[:, last_cols(z)], bx_hbm.at[last, :, 0:W], bx_send.at[last % RX], bx_recv.at[last % RX], partner)
+        return send(b_hbm.at[:, last_cols(z)], bx_hbm.at[last, :, 0:W], bx_send.at[last % 2], bx_recv.at[last % RX], partner)
 
     def last_bxz():
-        return send(bz_hbm.at[paired, :, 0:W], bxz_hbm.at[paired, :, 0:W], bxz_send.at[paired % RZ], bxz_recv.at[paired % RZ], partner)
+        return send(bz_hbm.at[paired, :, 0:W], bxz_hbm.at[paired, :, 0:W], bxz_send, bxz_recv.at[paired % RZ], partner)
 
     def last_piece(k):
         src = (b_hbm.at[:, last_cols(z)], bx_hbm.at[last, :, 0:W], bz_hbm.at[paired, :, 0:W], bxz_hbm.at[paired, :, 0:W])[k]
@@ -255,7 +261,7 @@
     last_part = pl.ds(0, upper)
 
     def last_sem(k):
-        return (r1_sem.at[last % 2, 1], rk_sem, r1_sem.at[last % 2, 0])[k]
+        return (r1_sem.at[last % 2, 1], ch_recv.at[1], r1_sem.at[last % 2, 0])[k]
 
     def last_send1(g, k):
         s = last % 2
@@ -291,11 +297,11 @@
         wait_bytes(q_v.at[t % DO], qs_sem.at[t % DO])
 
     def take(t, g, phase, slots, high):
-        when(t, slots, high, lambda: pl.semaphore_wait(credit.at[phase, g], 1))
+        when(t, slots, high, lambda: pl.semaphore_wait(credit.at[2 * phase + g], 1))
 
     def give(t, g, phase, axis, slots, high):
         when(t, 0, high - slots, lambda: pl.semaphore_signal(
-            credit.at[phase, g], inc=1, device_id=axis_nbr[axis], device_id_type=MESH))
+            credit.at[2 * phase + g], inc=1, device_id=axis_nbr[axis], device_id_type=MESH))
 
     for copy in own:
         copy.start()
@@ -321,7 +327,7 @@
         copy.start()
     for t in range(2):
         wait_bytes(b_v.at[t, pl.ds(0, 2 * depth)], b_sem.at[t])
-    wait_bytes(a_v.at[0], own_sem)
+    wait_bytes(a_v.at[0], ch_recv.at[14])
     end_group(1, 4)
     first_two(3, lambda j: j + j // 2)
     for h in both:
@@ -344,8 +350,8 @@
 
     def start_late():
         def body(t, carry):
-            for g in both:
-                when(t, D3, plain, lambda g=g: pl.semaphore_wait(credit.at[2, g], 1))
+            take(t, 0, 2, D3, plain)
+            for g in both:
                 send3(t, g).start()
             return carry
 
@@ -359,21 +365,23 @@
         lax.fori_loop(low, high, body, 0)
 
     def end_hops():
-        wait_bytes(a_v.at[pl.ds(0, hops // 4)], hop_send)
+        wait_bytes(a_v.at[pl.ds(0, hops // 4)], qr_sem)
         for n in range(AHEAD):
             a_chunk(n).wait_send()
 
     def step(i, carry):
         t = i
+        when(t, LAG, LAG + 1, end_hops)
+        when(t, LAG, tiles + 3, lambda: end_chunks(t - LAG))
         when(t, 0, tiles, lambda: start_chunks(t))
-        when(t, LAG, tiles + 3, lambda: end_chunks(t - LAG))
-        when(t, 1, tiles + 1, lambda: bx_copy(t - 1).wait_send())
-        when(t, plain + 1, tiles + 1, lambda: bxz_copy(t - 1 - plain).wait_send())
-        when(t, LAG, LAG + 1, end_hops)
+        when(t, 1, tiles - 1, lambda: fetch_near(t + 1))
+        when(t, tiles - 1, tiles, last_near)
+        when(t, 0, 1, lambda: bx_copy(0).wait_send())
+        when(t, 0, tiles - 1, lambda: bx_copy(t + 1).wait_send())
+        when(t, tiles - 1, tiles, lambda: last_bx().wait_send())
+        when(t, plain, tiles, lambda: bxz_copy(t - plain).wait_send())
         when(t, 0, tiles - LOOK, lambda: bx_copy(t + LOOK).start())
         when(t, tiles - LOOK, tiles - LOOK + 1, lambda: last_bx().start())
-        when(t, 1, tiles - 1, lambda: fetch_near(t + 1))
-        when(t, tiles - 1, tiles, last_near)
         when(t, 2, tiles + 2, lambda: sent1(t - 2))
 
         def wait_b(pieces):
@@ -392,7 +400,7 @@
             last_partials()
 
             for g in both:
-                pl.semaphore_wait(credit.at[0, g], 1)
+                pl.semaphore_wait(credit.at[g], 1)
                 last_send1(g, 0).start()
 
         def start_kept():
@@ -426,7 +434,7 @@
         def last1():
             last_add1(0)
             for g in both:
-                pl.semaphore_wait(credit.at[1, g], 1)
+                pl.semaphore_wait(credit.at[2 + g], 1)
                 send2(last, g, 1, upper).start()
             for g in both:
                 send2(last - 1, g, 0).start()
@@ -465,7 +473,6 @@
             each(plain - LATE, plain, sent3)
             each(tiles + 3 - LAG, tiles, end_chunks)
             each(max(plain, last + 1 - DO), tiles - 1, pair_sent)
-            last_bx().wait_send()
             last_bxz().wait_send()
             add2_here(last - 1)
             last_add1(2)
@@ -492,8 +499,8 @@
         when(t2, plain + DO, last + 1, lambda: pair_sent(t2 - DO))
         when(t2, 0, plain, lambda: add2(1))
         when(t2, plain, tiles, add2_there)
-        for g in both:
-            take(t2, g, 2, D3, plain - LATE)
+        take(t2, 0, 2, D3, plain - LATE)
+        for g in both:
             when(t2, 0, plain - LATE, lambda g=g: send3(t2, g).start())
             when(t2, plain, tiles, lambda g=g: pair_there(t2, g).start())
         when(t2, 0, plain, lambda: add2(0))
@@ -506,7 +513,7 @@
         when(t3, 0, plain - LATE, lambda: got3(t3))
         for g in both:
             when(t3, 0, plain - LATE, lambda g=g: add3(t3, g))
-            give(t3, g, 2, AZ, D3, plain)
+        give(t3, 0, 2, AZ, D3, plain)
         when(t, last - 2, last - 1, start_late)
         when(t, plain - 1, tiles - 1, lambda: fetch_last(t + 1))
         when(t, tiles - 1, tiles, last_fetch)
@@ -554,9 +561,9 @@
                 pltpu.VMEM((D3, 2, 2, rows, W), f32),
                 pltpu.VMEM((D3, 2, rows, W), f32),
                 pltpu.VMEM((DO, 2, rows, W), bf16),
-                dma, dma, dma((RX,)), dma((RX,)), dma((RZ,)), dma((RZ,)), dma((RC,)), dma((max(2 + paired, 14),)), dma((2,)),
-                dma((2,)), dma((2, 2)), dma, dma((2,)), dma((2, 2)), dma((D3,)), dma((D3,)), dma((DO,)), dma,
-                pltpu.SemaphoreType.REGULAR((3, 2)),
+                dma((2,)), dma((RX,)), dma, dma((RZ,)), dma((5 * pace(columns) // 100 + 2,)), dma((max(2 + paired, 15),)), dma((2,)),
+                dma((2,)), dma((2, 2)), dma((2,)), dma((2, 2)), dma((D3,)), dma((D3,)), dma((DO,)), dma,
+                pltpu.SemaphoreType.REGULAR((5,)),
             ],
             compiler_params=pltpu.CompilerParams(
                 collective_id=0, has_side_effects=True, vmem_limit_bytes=56 * 1024 * 1024),

time: 888 us -> 888 us (level)
  no operation moved by 1% of the time
where the time goes in v7:
time: 888 us
  Pallas kernels  885 us (100%)
    pallas_call x1, Pallas kernels, local_block(): pl.pallas_call(kernel, name='matmul_reduce_scatter', out_shape=(pltpu.VME...  885 us

profile of v7, /device:TPU:0, one launch (start us, length us, event | category | flops | bytes accessed | tf_op | source)
XLA Modules:
  0.0 888.1 jit_solution(13582104068906776000)
XLA Ops:
  0.0 885.1 %matmul_reduce_scatter.1 = (bf16[256,14336]{1,0:T(8,128)(2,1)S(1)}, bf16[42,2048,256]{2,1,0:T(8,128)(2,1)}, bf16[15,2048,256]{2,1,0:T(8,128)(2,1)}, bf16[15,2048,256]{2,1,0:T(8,128)(2,1)}, bf16[2,256,4096]{2,1,0:T(8,128)(2,1)}) custom-call(bf16[256,32768]{1,0:T(8,128)(2,1)} %a_hbm.1, bf16[2048,14336]{1,0:T(8,128)(2,1)} %b_hbm.1), custom_call_target="tpu_custom_call" | custom-call | flops 240518168576 | bytes 176160768 | tf_op jit(solution)/shard_map/matmul_reduce_scatter/pallas_call | solution.py:542
  885.1 3.1 copy.4

commit v8 on v7

--- a/solution.py
+++ b/solution.py
@@ -476,6 +476,11 @@
             last_bxz().wait_send()
             add2_here(last - 1)
             last_add1(2)
+            pair_sent(last - 1)
+            sent2(last - 1)
+            wait_bytes(r1_v.at[last % 2, :, :, last_part], s1_sem.at[last % 2])
+            wait_bytes(q_v.at[last % DO, :, last_part], qs_sem.at[last % DO])
+            wait_bytes(c_v.at[:, pl.ds(0, paired * C + W)], qr_sem)
             got2(last, 0, upper)
             for g in both:
                 c_v[pl.ds(g * upper, upper), last_cols(z)] = sum2(last, g, 0, upper).astype(jnp.bfloat16)
@@ -521,12 +526,7 @@
 
     lax.fori_loop(0, tiles + 3, step, 0)
 
-    each(max(plain, tiles - 1), tiles, pair_sent)
-    wait_bytes(r1_v.at[last % 2, :, :, last_part], s1_sem.at[last % 2])
-    sent2(last - 1)
     sent2(last, upper)
-    wait_bytes(q_v.at[last % DO, :, pl.ds(0, upper)], qs_sem.at[last % DO])
-    wait_bytes(c_v.at[:, pl.ds(0, paired * C + W)], qr_sem)
 
 
 def solution(mesh):

time: 888 us -> 888 us (level)
  no operation moved by 1% of the time
where the time goes in v8:
time: 888 us
  Pallas kernels  885 us (100%)
    pallas_call x1, Pallas kernels, local_block(): pl.pallas_call(kernel, name='matmul_reduce_scatter', out_shape=(pltpu.VME...  885 us

profile of v8, /device:TPU:0, one launch (start us, length us, event | category | flops | bytes accessed | tf_op | source)
XLA Modules:
  0.0 888.1 jit_solution(8257795668055941189)
XLA Ops:
  0.0 885.1 %matmul_reduce_scatter.1 = (bf16[256,14336]{1,0:T(8,128)(2,1)S(1)}, bf16[42,2048,256]{2,1,0:T(8,128)(2,1)}, bf16[15,2048,256]{2,1,0:T(8,128)(2,1)}, bf16[15,2048,256]{2,1,0:T(8,128)(2,1)}, bf16[2,256,4096]{2,1,0:T(8,128)(2,1)}) custom-call(bf16[256,32768]{1,0:T(8,128)(2,1)} %a_hbm.1, bf16[2048,14336]{1,0:T(8,128)(2,1)} %b_hbm.1), custom_call_target="tpu_custom_call" | custom-call | flops 240518168576 | bytes 176160768 | tf_op jit(solution)/shard_map/matmul_reduce_scatter/pallas_call | solution.py:542
  885.1 3.1 copy.4
